TPU v7x, 256 devices: a whole 4x4x8 slice. The times are simulated.
256 devices in a mesh: expert: 8 (over y, core), shard: 32 (over z, x).
Axes of the slice: x: 4, y: 4, z: 8, core: 2. Of those that a mesh axis runs over, the one named last changes fastest.
Arguments:
- master_down: float32 [16, 6400, 4096], P('expert', None, 'shard'), may hold values from -0.15625 to 0.15625
- second_down: bfloat16 [16, 6400, 4096], P('expert', None, 'shard'), may hold values from -0.0390625 to 0.0390625
- router_weight: float32 [4096, 16], P('shard', 'expert'), may hold values from -0.09375 to 0.09375
- router_gain: float32 [4096], P('shard'), may hold values from 0.25 to 1.75
Outputs:
- final_down: bfloat16 [16, 6400, 4096], P('expert', 'shard')
- scale_down: float32 [16, 6400], P('expert', 'shard')
- serve_router: bfloat16 [4096, 16], replicated
All inputs are finite; a program needn't handle non-finite values.
Results may differ from a plain program's by a relative error of at most 0.0085.
Values may be sent and summed in bfloat16 or wider, within the bound.
No kernel may reach another device: no remote copies, remote signals or barrier semaphores. Data moves between devices by JAX's collectives and lax.ppermute only.
A program may use at most 64 MiB of HBM per device.

v0:
```python
import jax
import jax.numpy as jnp
from jax import lax
from jax.sharding import PartitionSpec as P


def sent_to_all(x, axis):
    count = lax.axis_size(axis)
    return lax.all_to_all(jnp.broadcast_to(x[None], (count, *x.shape)), axis, 0, 0, tiled=True)


def taken_together(x, axis):
    everything = sent_to_all(x, axis)
    return jnp.sum(everything.astype(jnp.float32), axis=0)


def laid_out(parts, dim):
    dims = list(parts.shape[1:])
    dims[dim] *= parts.shape[0]
    return jnp.moveaxis(parts, 0, dim).reshape(dims)


def gathered_copies(x, axis, dim):
    parts = sent_to_all(x, axis)
    return laid_out(parts, dim)


def body(master_down, second_down, router_weight, router_gain):
    merged_down = master_down + second_down.astype(jnp.float32)
    total_down = taken_together(
        jnp.sum(merged_down * merged_down, axis=2).astype(jnp.bfloat16), "shard"
    ).astype(jnp.float32)
    scale_down = jnp.sqrt(total_down)
    narrow_down = (merged_down / jnp.expand_dims(scale_down, 2)).astype(jnp.bfloat16)
    final_down = lax.all_to_all(narrow_down, "shard", split_axis=1, concat_axis=2, tiled=True)
    scale_down = lax.dynamic_slice_in_dim(
        scale_down, lax.axis_index("shard") * final_down.shape[1], final_down.shape[1], axis=1
    )
    part_router = (router_weight * router_gain[:, None]).astype(jnp.bfloat16)
    row_router = gathered_copies(part_router, "shard", 0)
    serve_router = gathered_copies(row_router, "expert", 1)
    return (final_down, scale_down, serve_router)


def solution(mesh):
    placed = (
        P("expert", None, "shard"),
        P("expert", None, "shard"),
        P("shard", "expert"),
        P("shard"),
    )
    return jax.shard_map(
        body,
        mesh=mesh,
        in_specs=placed,
        out_specs=(P("expert", "shard", None), P("expert", "shard"), P()),
        check_vma=False,
    )
```

profile of v0, /device:TPU:3, one launch (start us, length us, event | category | flops | bytes accessed | tf_op | source)
XLA Modules:
  0.0 183.1 jit_solution(7028451042214102554)
XLA Ops:
  0.6 0.7 multiply_convert_fusion
  1.3 0.6 broadcast_in_dim.9
  1.9 11.1 %all-to-all-start.2 = ((bf16[32,128,2]{1,2,0:T(2,128)(2,1)}), bf16[32,128,2]{1,2,0:T(2,128)(2,1)S(1)}, u32[]{:S(2)}, u32[]{:S(2)}) async-start(bf16[32,128,2]{1,2,0:T(2,128)(2,1)} %broadcast_in_dim.9), calls=%async_computation.2 | async-start | bytes 32768 | tf_op jit(solution)/shard_map/all_to_all | solution.py:9
  13.0 0.0 copy-start
  13.0 5.7 %multiply_reduce_fusion = bf16[2,6400]{1,0:T(2,128)(2,1)S(1)} fusion(f32[2,6400,128]{2,1,0:T(8,128)} %param.4, bf16[2,6400,128]{2,1,0:T(8,128)(2,1)} %param.5), kind=kLoop, calls=%fused_computation.1 | loop fusion | flops 6540800 | bytes 9856000 | tf_op jit(solution)/shard_map/reduce_sum | solution.py:31
  18.8 1.8 %all-to-all-done.2 = bf16[32,128,2]{1,2,0:T(2,128)(2,1)S(1)} async-done(((bf16[32,128,2]{1,2,0:T(2,128)(2,1)}), bf16[32,128,2]{1,2,0:T(2,128)(2,1)S(1)}, u32[]{:S(2)}, u32[]{:S(2)}) %all-to-all-start.2) | async-done | bytes 16416 | tf_op jit(solution)/shard_map/all_to_all | solution.py:9
  20.6 0.4 broadcast_in_dim.8
  21.0 29.0 %all_to_all.33 = bf16[32,2,6400]{2,1,0:T(2,128)(2,1)} all-to-all(bf16[32,2,6400]{2,1,0:T(2,128)(2,1)S(1)} %broadcast_in_dim.8), channel_id=1, replica_groups=mesh['expert'=8,'shard'=32] {'shard'}, dimensions={0} | all-to-all | bytes 1638400 | tf_op jit(solution)/shard_map/all_to_all | solution.py:9
  50.1 0.7 broadcast_in_dim.11
  50.8 7.1 %all-to-all-start.3 = ((bf16[8,4096,2]{1,2,0:T(2,128)(2,1)}), bf16[8,4096,2]{1,2,0:T(2,128)(2,1)S(1)}, u32[]{:S(2)}, u32[]{:S(2)}) async-start(bf16[8,4096,2]{1,2,0:T(2,128)(2,1)} %broadcast_in_dim.11), calls=%async_computation.3 | async-start | bytes 262144 | tf_op jit(solution)/shard_map/all_to_all | solution.py:9
  57.9 1.3 convert_reduce_fusion
  59.2 0.1 sqrt.7
  59.3 0.0 copy-done
  59.3 4.7 %divide_convert_fusion = bf16[2,6400,128]{2,1,0:T(8,128)(2,1)S(1)} fusion(f32[2,6400,128]{2,1,0:T(8,128)} %param.4, bf16[2,6400,128]{2,1,0:T(8,128)(2,1)S(1)} %copy-done, f32[2,6400]{1,0:T(2,128)S(1)} %sqrt.7), kind=kLoop, calls=%fused_computation | loop fusion | flops 6553600 | bytes 13158400 | tf_op jit(solution)/shard_map/convert_element_type | solution.py:34
  64.1 27.9 %copy.31 = bf16[2,6400,128]{2,0,1:T(2,128)(2,1)} copy(bf16[2,6400,128]{2,1,0:T(8,128)(2,1)S(1)} %divide_convert_fusion) | data formatting | bytes 6553600 | tf_op jit(solution)/shard_map/convert_element_type | solution.py:34
  91.9 0.0 all-to-all-done.3
  91.9 5.0 %all-to-all-start.1 = ((bf16[2,6400,128]{2,0,1:T(2,128)(2,1)}), bf16[2,6400,128]{2,0,1:T(2,128)(2,1)S(1)}, u32[]{:S(2)}, u32[]{:S(2)}) async-start(bf16[2,6400,128]{2,0,1:T(2,128)(2,1)} %copy.31), calls=%async_computation.1 | async-start | bytes 6553600 | tf_op jit(solution)/shard_map/all_to_all | solution.py:35
  97.0 0.7 reshape.18
  97.7 0.7 constant_dynamic-slice_fusion
  98.3 76.1 %all-to-all-done.1 = bf16[2,6400,128]{2,0,1:T(2,128)(2,1)S(1)} async-done(((bf16[2,6400,128]{2,0,1:T(2,128)(2,1)}), bf16[2,6400,128]{2,0,1:T(2,128)(2,1)S(1)}, u32[]{:S(2)}, u32[]{:S(2)}) %all-to-all-start.1) | async-done | bytes 3276832 | tf_op jit(solution)/shard_map/all_to_all | solution.py:35
  174.4 2.5 %copy.32 = bf16[2,200,32,128]{3,2,1,0:T(8,128)(2,1)} copy(bf16[2,200,32,128]{3,0,1,2:T(2,128)(2,1)S(1)} %bitcast.9) | data formatting | bytes 6553600 | tf_op jit(solution)/shard_map/all_to_all | solution.py:35
  176.9 6.2 %all_to_all.26 = bf16[2,200,4096]{2,1,0:T(8,128)(2,1)} reshape(bf16[2,200,32,128]{3,2,1,0:T(8,128)(2,1)} %copy.32) | data formatting | bytes 6553600 | tf_op jit(solution)/shard_map/all_to_all | solution.py:35
Async XLA Ops:
  1.9 18.7 %all-to-all-start.2 = ((bf16[32,128,2]{1,2,0:T(2,128)(2,1)}), bf16[32,128,2]{1,2,0:T(2,128)(2,1)S(1)}, u32[]{:S(2)}, u32[]{:S(2)}) async-start(bf16[32,128,2]{1,2,0:T(2,128)(2,1)} %broadcast_in_dim.9), calls=%async_computation.2 | async-start | bytes 32768 | tf_op jit(solution)/shard_map/all_to_all | solution.py:9
  13.0 46.3 %copy-start = (bf16[2,6400,128]{2,1,0:T(8,128)(2,1)S(1)}, bf16[2,6400,128]{2,1,0:T(8,128)(2,1)}, u32[]{:S(2)}) copy-start(bf16[2,6400,128]{2,1,0:T(8,128)(2,1)} %param.5) | copy-start | bytes 9830404
  50.8 41.1 %all-to-all-start.3 = ((bf16[8,4096,2]{1,2,0:T(2,128)(2,1)}), bf16[8,4096,2]{1,2,0:T(2,128)(2,1)S(1)}, u32[]{:S(2)}, u32[]{:S(2)}) async-start(bf16[8,4096,2]{1,2,0:T(2,128)(2,1)} %broadcast_in_dim.11), calls=%async_computation.3 | async-start | bytes 262144 | tf_op jit(solution)/shard_map/all_to_all | solution.py:9
  91.9 82.5 %all-to-all-start.1 = ((bf16[2,6400,128]{2,0,1:T(2,128)(2,1)}), bf16[2,6400,128]{2,0,1:T(2,128)(2,1)S(1)}, u32[]{:S(2)}, u32[]{:S(2)}) async-start(bf16[2,6400,128]{2,0,1:T(2,128)(2,1)} %copy.31), calls=%async_computation.1 | async-start | bytes 6553600 | tf_op jit(solution)/shard_map/all_to_all | solution.py:35
where the time goes:
time: 184 us; the launch traced here: 183 us
  waiting for transfers between devices  77.9 us (42%)
  local copies, waits for them, and re-layouts  39.8 us (22%)
  blocking collectives  29 us (16%)
  starting transfers between devices  23.2 us (13%)
  other arithmetic  12.5 us (7%)
    all_to_all x1, waiting for transfers between devices, body(): lax.all_to_all(narrow_down, 'shard', split_axis=1, concat_axis=2, tiled=T...  76.1 us
    all_to_all x1, blocking collectives, sent_to_all(): lax.all_to_all(jnp.broadcast_to(x[None], (count, *x.shape)), axis, 0, 0,...  29 us
    convert_element_type x1, local copies, waits for them, and re-layouts, body(): (merged_down / jnp.expand_dims(scale_down, 2)).astype(jnp.bfloat16)  27.9 us
    all_to_all x2, starting transfers between devices, sent_to_all(): lax.all_to_all(jnp.broadcast_to(x[None], (count, *x.shape)), axis, 0, 0,...  18.2 us
    all_to_all x2, local copies, waits for them, and re-layouts, body(): lax.all_to_all(narrow_down, 'shard', split_axis=1, concat_axis=2, tiled=T...  8.72 us
    reduce_sum x1, other arithmetic, body(): jnp.sum(merged_down * merged_down, axis=2).astype(jnp.bfloat16)  5.75 us
    all_to_all x1, starting transfers between devices, body(): lax.all_to_all(narrow_down, 'shard', split_axis=1, concat_axis=2, tiled=T...  5.01 us
    convert_element_type x1, other arithmetic, body(): (merged_down / jnp.expand_dims(scale_down, 2)).astype(jnp.bfloat16)  4.74 us
  transfers between devices with their start and end apart: 3, of which 2 were waited for; matrix products, arithmetic and copies ran while one was open for 22% of the time, Pallas kernels for 0%

commit v1 on v0

--- a/solution.py
+++ b/solution.py
@@ -32,7 +32,12 @@
     ).astype(jnp.float32)
     scale_down = jnp.sqrt(total_down)
     narrow_down = (merged_down / jnp.expand_dims(scale_down, 2)).astype(jnp.bfloat16)
-    final_down = lax.all_to_all(narrow_down, "shard", split_axis=1, concat_axis=2, tiled=True)
+    final_down = jnp.concatenate(
+        lax.all_to_all(
+            jnp.stack(jnp.split(narrow_down, lax.axis_size("shard"), axis=1)), "shard", 0, 0
+        ),
+        axis=2,
+    )
     scale_down = lax.dynamic_slice_in_dim(
         scale_down, lax.axis_index("shard") * final_down.shape[1], final_down.shape[1], axis=1
     )

time: 184 us -> 152 us (0.83)
  local copies, waits for them, and re-layouts: 39.8 us -> 7.59 us
    convert_element_type x1 -> x0, local copies, waits for them, and re-layouts: 27.9 us -> none  [body(): (merged_down / jnp.expand_dims(scale_down, 2)).astype(jnp.bfloat16)]
    all_to_all x2 -> x0, local copies, waits for them, and re-layouts: 8.72 us -> none  [body(): lax.all_to_all(narrow_down, 'shard', split_axis=1, concat_axis=2, tiled=T...]
    unnamed x2 -> x35, local copies, waits for them, and re-layouts: 0.01 us -> 2.25 us
    reshape x0 -> x1, local copies, waits for them, and re-layouts: none -> 2.14 us  [body(): jnp.concatenate(lax.all_to_all(jnp.stack(jnp.split(narrow_down, lax.axis_...]
  transfers between devices with their start and end apart: 3 -> 3, of which waited for: 2 -> 2; matrix products, arithmetic and copies ran while one was open for 22% -> 9% of each run, Pallas kernels for 0% -> 0%
where the time goes in v1:
time: 152 us; the launch traced here: 151 us
  waiting for transfers between devices  78.1 us (51%)
  blocking collectives  29 us (19%)
  starting transfers between devices  23.2 us (15%)
  other arithmetic  12.4 us (8%)
  local copies, waits for them, and re-layouts  7.59 us (5%)
    all_to_all x1, waiting for transfers between devices, body(): lax.all_to_all(jnp.stack(jnp.split(narrow_down, lax.axis_size('shard'), a...  76.1 us
    all_to_all x1, blocking collectives, sent_to_all(): lax.all_to_all(jnp.broadcast_to(x[None], (count, *x.shape)), axis, 0, 0,...  29 us
    all_to_all x2, starting transfers between devices, sent_to_all(): lax.all_to_all(jnp.broadcast_to(x[None], (count, *x.shape)), axis, 0, 0,...  18.2 us
    reduce_sum x1, other arithmetic, body(): jnp.sum(merged_down * merged_down, axis=2).astype(jnp.bfloat16)  5.6 us
    all_to_all x1, starting transfers between devices, body(): lax.all_to_all(jnp.stack(jnp.split(narrow_down, lax.axis_size('shard'), a...  5.01 us
    convert_element_type x1, other arithmetic, body(): (merged_down / jnp.expand_dims(scale_down, 2)).astype(jnp.bfloat16)  4.74 us
  transfers between devices with their start and end apart: 3, of which 2 were waited for; matrix products, arithmetic and copies ran while one was open for 9% of the time, Pallas kernels for 0%

profile of v1, /device:TPU:3, one launch (start us, length us, event | category | flops | bytes accessed | tf_op | source)
XLA Modules:
  0.0 151.1 jit_solution(17886167564966132452)
XLA Ops:
  0.6 0.7 multiply_convert_fusion
  1.3 0.6 broadcast_in_dim.9
  1.9 11.1 %all-to-all-start.2 = ((bf16[32,128,2]{1,2,0:T(2,128)(2,1)}), bf16[32,128,2]{1,2,0:T(2,128)(2,1)S(1)}, u32[]{:S(2)}, u32[]{:S(2)}) async-start(bf16[32,128,2]{1,2,0:T(2,128)(2,1)} %broadcast_in_dim.9), calls=%async_computation.2 | async-start | bytes 32768 | tf_op jit(solution)/shard_map/all_to_all | solution.py:9
  13.0 5.6 %multiply_reduce_fusion = bf16[2,6400]{1,0:T(2,128)(2,1)S(1)} fusion(f32[2,6400,128]{2,1,0:T(8,128)} %param.4, bf16[2,6400,128]{2,1,0:T(8,128)(2,1)} %param.5), kind=kLoop, calls=%fused_computation.1 | loop fusion | flops 6540800 | bytes 9856000 | tf_op jit(solution)/shard_map/reduce_sum | solution.py:31
  18.6 0.0 copy-start
  18.6 2.0 %all-to-all-done.2 = bf16[32,128,2]{1,2,0:T(2,128)(2,1)S(1)} async-done(((bf16[32,128,2]{1,2,0:T(2,128)(2,1)}), bf16[32,128,2]{1,2,0:T(2,128)(2,1)S(1)}, u32[]{:S(2)}, u32[]{:S(2)}) %all-to-all-start.2) | async-done | bytes 16416 | tf_op jit(solution)/shard_map/all_to_all | solution.py:9
  20.6 0.4 broadcast_in_dim.8
  21.0 29.0 %all_to_all.20 = bf16[32,2,6400]{2,1,0:T(2,128)(2,1)} all-to-all(bf16[32,2,6400]{2,1,0:T(2,128)(2,1)S(1)} %broadcast_in_dim.8), channel_id=1, replica_groups=mesh['expert'=8,'shard'=32] {'shard'}, dimensions={0} | all-to-all | bytes 1638400 | tf_op jit(solution)/shard_map/all_to_all | solution.py:9
  50.0 0.7 broadcast_in_dim.11
  50.8 7.1 %all-to-all-start.3 = ((bf16[8,4096,2]{1,2,0:T(2,128)(2,1)}), bf16[8,4096,2]{1,2,0:T(2,128)(2,1)S(1)}, u32[]{:S(2)}, u32[]{:S(2)}) async-start(bf16[8,4096,2]{1,2,0:T(2,128)(2,1)} %broadcast_in_dim.11), calls=%async_computation.3 | async-start | bytes 262144 | tf_op jit(solution)/shard_map/all_to_all | solution.py:9
  57.9 1.3 convert_reduce_fusion
  59.2 0.1 sqrt.7
  59.3 0.0 copy-done
  59.3 4.7 %divide_convert_fusion = bf16[2,6400,128]{2,1,0:T(8,128)(2,1)S(1)} fusion(f32[2,6400,128]{2,1,0:T(8,128)} %param.4, bf16[2,6400,128]{2,1,0:T(8,128)(2,1)S(1)} %copy-done, f32[2,6400]{1,0:T(2,128)S(1)} %sqrt.7), kind=kLoop, calls=%fused_computation | loop fusion | flops 6553600 | bytes 13158400 | tf_op jit(solution)/shard_map/convert_element_type | solution.py:34
  64.8 0.0 copy-start.1
  64.8 1.7 %copy-done.1 = bf16[32,2,200,128]{3,2,1,0:T(8,128)(2,1)} copy-done((bf16[32,2,200,128]{3,2,1,0:T(8,128)(2,1)}, bf16[32,2,200,128]{3,2,1,0:T(8,128)(2,1)S(1)}, u32[]{:S(2)}) %copy-start.1) | copy-done | bytes 3276824
  66.5 0.0 all-to-all-done.3
  66.5 5.0 %all-to-all-start.1 = ((bf16[32,2,200,128]{3,2,1,0:T(8,128)(2,1)}), bf16[32,2,200,128]{3,2,1,0:T(8,128)(2,1)S(1)}, u32[]{:S(2)}, u32[]{:S(2)}) async-start(bf16[32,2,200,128]{3,2,1,0:T(8,128)(2,1)} %copy-done.1), calls=%async_computation.1 | async-start | bytes 6553600 | tf_op jit(solution)/shard_map/all_to_all | solution.py:36
  71.5 0.7 reshape.26
  72.3 0.7 constant_dynamic-slice_fusion
  72.9 76.1 %all-to-all-done.1 = bf16[32,2,200,128]{3,2,1,0:T(8,128)(2,1)S(1)} async-done(((bf16[32,2,200,128]{3,2,1,0:T(8,128)(2,1)}), bf16[32,2,200,128]{3,2,1,0:T(8,128)(2,1)S(1)}, u32[]{:S(2)}, u32[]{:S(2)}) %all-to-all-start.1) | async-done | bytes 3276832 | tf_op jit(solution)/shard_map/all_to_all | solution.py:36
  149.0 2.1 %copy_bitcast_fusion = bf16[2,200,4096]{2,1,0:T(8,128)(2,1)} fusion(bf16[32,2,200,128]{3,2,1,0:T(8,128)(2,1)S(1)} %all-to-all-done.1), kind=kLoop, calls=%fused_computation.3 | loop fusion | bytes 6553600 | tf_op jit(solution)/shard_map/reshape | solution.py:35
  (32 shorter events, 0.6 us)
Async XLA Ops:
  1.9 18.7 %all-to-all-start.2 = ((bf16[32,128,2]{1,2,0:T(2,128)(2,1)}), bf16[32,128,2]{1,2,0:T(2,128)(2,1)S(1)}, u32[]{:S(2)}, u32[]{:S(2)}) async-start(bf16[32,128,2]{1,2,0:T(2,128)(2,1)} %broadcast_in_dim.9), calls=%async_computation.2 | async-start | bytes 32768 | tf_op jit(solution)/shard_map/all_to_all | solution.py:9
  18.6 40.7 %copy-start = (bf16[2,6400,128]{2,1,0:T(8,128)(2,1)S(1)}, bf16[2,6400,128]{2,1,0:T(8,128)(2,1)}, u32[]{:S(2)}) copy-start(bf16[2,6400,128]{2,1,0:T(8,128)(2,1)} %param.5) | copy-start | bytes 9830404
  50.8 15.8 %all-to-all-start.3 = ((bf16[8,4096,2]{1,2,0:T(2,128)(2,1)}), bf16[8,4096,2]{1,2,0:T(2,128)(2,1)S(1)}, u32[]{:S(2)}, u32[]{:S(2)}) async-start(bf16[8,4096,2]{1,2,0:T(2,128)(2,1)} %broadcast_in_dim.11), calls=%async_computation.3 | async-start | bytes 262144 | tf_op jit(solution)/shard_map/all_to_all | solution.py:9
  64.8 1.7 %copy-start.1 = (bf16[32,2,200,128]{3,2,1,0:T(8,128)(2,1)}, bf16[32,2,200,128]{3,2,1,0:T(8,128)(2,1)S(1)}, u32[]{:S(2)}) copy-start(bf16[32,2,200,128]{3,2,1,0:T(8,128)(2,1)S(1)} %fusion) | copy-start | bytes 9830404
  66.5 82.5 %all-to-all-start.1 = ((bf16[32,2,200,128]{3,2,1,0:T(8,128)(2,1)}), bf16[32,2,200,128]{3,2,1,0:T(8,128)(2,1)S(1)}, u32[]{:S(2)}, u32[]{:S(2)}) async-start(bf16[32,2,200,128]{3,2,1,0:T(8,128)(2,1)} %copy-done.1), calls=%async_computation.1 | async-start | bytes 6553600 | tf_op jit(solution)/shard_map/all_to_all | solution.py:36
